TPU v7x, 256 devices: a whole 4x4x8 slice. The times are simulated.
256 devices in a mesh: gx: 32 (over z, y_lo, core), gy: 8 (over y_hi, x).
Axes of the slice: x: 4, y: 4 (y_hi: 2, y_lo: 2; y = y_hi * 2 + y_lo), z: 8, core: 2. Of those that a mesh axis runs over, the one named last changes fastest.
Arguments:
- right_side: float32 [32, 8, 512, 256], P('gx', 'gy'), may hold values from -8 to 8, as said below
- coords: float32 [32, 8, 2, 512], P('gx', 'gy'), may hold values from 0 to 1
- noise: float32 [32, 8, 512], P('gx', 'gy'), may hold values from 0.25 to 1
- intersect: int32 [32, 8, 128], P('gx', 'gy'), may hold values from 0 to 4607, as said below
Outputs:
- solution: float32 [32, 8, 512, 256], P('gx', 'gy')
- residual: float32 [32, 8, 512, 256], P('gx', 'gy')
Inputs may be any that keep to these rules, and one draw needn't show every extreme that they name: `right_side`: right-hand sides of order one. `intersect`: each subdomain's list holds 128 distinct indices in increasing order; none names the subdomain itself (block number 4) or a subdomain beyond the first or last one along the second dimension.
All inputs are finite; a program needn't handle non-finite values.
Results may differ from a plain program's by a relative error of at most 0.0003.
Values sent between devices are 32-bit elements; how exact they have to be, the bound alone decides.
A program may use at most 128 MiB of HBM per device.

v0:
```python
import functools
import math

import jax
import jax.numpy as jnp
from jax import lax
from jax.experimental import pallas as pl
from jax.experimental.pallas import tpu as pltpu
from jax.sharding import PartitionSpec as P

MESH = pl.DeviceIdType.MESH
HIGH = lax.Precision.HIGHEST
F32 = jnp.float32
BF16 = jnp.bfloat16
SCALE = math.sqrt(3.0) / 0.25
LEAST_NOISE = 0.25
NEWTON_STEPS = 7
LANES = 128
NEAR = [(a, b) for a in (-1, 0, 1) for b in (-1, 0, 1) if (a, b) != (0, 0)]
BOTH = (1, -1)


def slot(a, b):
    return (a + 1) * 3 + (b + 1)


def kernel_values(target_x, target_y, source_x, source_y):
    dx = target_x - source_x
    dy = target_y - source_y
    square = dx * dx + dy * dy
    distance = square * lax.rsqrt(jnp.maximum(square, 1e-30))
    scaled = SCALE * distance
    clipped = jnp.minimum(distance, 1.0)
    left = 1.0 - clipped
    square = left * left
    return (1.0 + scaled) * jnp.exp(-scaled) * (square * square * (4.0 * clipped + 1.0))


def halves(value):
    high = value.astype(BF16)
    low = (value - high.astype(F32)).astype(BF16)
    return high, low


def packed(value):
    return jnp.concatenate(halves(value), axis=1)


def bf_dot(left, right):
    return jnp.dot(left, right, preferred_element_type=F32)


def split_dot(high, low, both):
    first = bf_dot(high, both)
    return first[:, :LANES] + first[:, LANES:] + bf_dot(low, both[:, :LANES])


def pick_dot(chosen, both):
    first = bf_dot(chosen, both)
    return first[:, :LANES] + first[:, LANES:]


def three_dot(left, right):
    (left_high, left_low), (right_high, right_low) = halves(left), halves(right)
    return bf_dot(left_high, right_high) + bf_dot(left_high, right_low) + bf_dot(left_low, right_high)


def full_dot(left, right, dims=((1,), (0,))):
    return lax.dot_general(left, right, (dims, ((), ())), precision=HIGH, preferred_element_type=F32)


def identity(size):
    row = lax.broadcasted_iota(jnp.int32, (size, size), 0)
    return (row == lax.broadcasted_iota(jnp.int32, (size, size), 1)).astype(F32)


def newton_inverse(matrix, result):
    size = matrix.shape[0]
    value = matrix[...]
    largest = jnp.max(jnp.sum(jnp.abs(value), axis=1, keepdims=True), axis=0, keepdims=True)
    alpha = 1.0 / largest
    least = LEAST_NOISE * alpha
    scale = 2.0 / (1.0 + least)
    first = scale * alpha
    result[...] = (2.0 * first) * identity(size) - (first * first) * value

    def step(dot, least):
        scale = 2.0 / (1.0 + least)
        current = result[...]
        product = dot(matrix[...], current)
        result[...] = scale * dot(current, 2.0 * identity(size) - scale * product)
        return 4.0 * least / ((1.0 + least) * (1.0 + least))

    least = lax.fori_loop(0, NEWTON_STEPS - 1, lambda _, least: step(three_dot, least),
                          4.0 * least / ((1.0 + least) * (1.0 + least)))
    step(full_dot, least)


def body(cfg, info_ref, b_ref, x_ref, r_ref, *scratch):
    ref = dict(zip(cfg["names"], scratch))
    points, ov = cfg["points"], cfg["ov"]
    ext = points + ov
    gx, gy = cfg["gx"], cfg["gy"]
    seat, col = lax.axis_index("gx"), lax.axis_index("gy")
    mid = gy // 2

    def trades(r, c):
        return (c // mid + r) % 2

    def host(r, c):
        return (r + trades(r, c) * (2 - 4 * ((r // 2) % 2)), c)

    row, _ = host(seat, col)
    traded, kept = trades(seat, col) == 1, trades(seat, col) == 0
    has = {0: None, 1: col < gy - 1, -1: col > 0, "traded": traded}
    send_sem, recv_sem = ref["send"], ref["recv"]
    counter = [0]
    pending = {0: [], 1: [], -1: [], "traded": []}
    latest = []

    def guarded(which, action):
        if which == 0:
            action()
        else:
            pl.when(has[which])(action)

    def device(a, b):
        return host((row + a + gx) % gx, (col + b + gy) % gy)

    def heir(a, b):
        return host((seat + a + gx) % gx, (col + b + gy) % gy)

    def holder(a, b):
        return ((row + a + gx) % gx, (col + b + gy) % gy)

    mate = (seat + 2 - 4 * ((seat // 2) % 2), col)

    def copy_to(src, dst, target):
        key = counter[0]
        counter[0] += 1
        return pltpu.make_async_remote_copy(
            src_ref=src, dst_ref=dst, send_sem=send_sem.at[key], recv_sem=recv_sem.at[key],
            device_id=target, device_id_type=MESH)

    def send(src, dst, a, b, guard=None, target=None):
        out = b if guard is None else guard
        arrives = -b if guard is None else guard
        desc = copy_to(src, dst, device(a, b) if target is None else target)
        guarded(out, desc.start)
        pending[out].append(desc)
        latest.append((out, desc))
        return functools.partial(guarded, arrives, desc.wait_recv)

    def sent(begin, end):
        for out, desc in latest[begin:end]:
            guarded(out, desc.wait_send)
            pending[out][:] = [other for other in pending[out] if other is not desc]

    info_all = ref["info_all"]
    for n in range(9):
        if n != 4:
            info_all[n] = jnp.full(info_all.shape[1:], -1.0, F32)

    @pl.when(kept)
    def _():
        info_all[4] = info_ref[...]

    @pl.when((col == 0) | (col == gy - 1))
    def _():
        for name in ("ret", "halo", "part_in", "take_in", "give_in"):
            buf = ref[name]
            flat = math.prod(buf.shape[:-2])
            for n in range(flat):
                index, rest = [], n
                for d in reversed(buf.shape[:-2]):
                    index.append(rest % d)
                    rest //= d
                buf[tuple(reversed(index))] = jnp.zeros(buf.shape[-2:], F32)

    groups = cfg["groups"]

    def partner(stride, many, columns_too, offset):
        position = (seat // stride) % many
        ahead = (position + offset % many) % many
        return (seat + (ahead - position) * stride, (col + offset // many) % gy if columns_too > 1 else col)

    barrier = pltpu.get_barrier_semaphore()
    for a, b in NEAR:
        for whom in (device, heir, holder):
            pl.semaphore_signal(barrier, inc=1, device_id=whom(a, b), device_id_type=MESH)
    pl.semaphore_signal(barrier, inc=1, device_id=mate, device_id_type=MESH)
    total = 3 * len(NEAR) + 1
    for group in groups:
        for offset in range(1, group[1] * group[2]):
            pl.semaphore_signal(barrier, inc=1, device_id=partner(*group, offset), device_id_type=MESH)
            total += 1
    pl.semaphore_wait(barrier, total)

    waits = [send(info_ref, info_all.at[slot(-a, -b)], a, b, target=heir(a, b)) for a, b in NEAR]
    waits.append(send(info_ref, info_all.at[4], 0, 0, guard="traded", target=mate))
    be = ref["be"]
    own = slice(0, points)

    def half(h):
        return slice(h * LANES, (h + 1) * LANES)

    came_right = [send(b_ref.at[:, half(h)], be.at[h, own], 0, 0, guard="traded", target=mate) for h in range(2)]

    @pl.when(kept)
    def _():
        for h in range(2):
            be[h, own] = b_ref[:, half(h)]

    for wait in waits:
        wait()

    gather, scatter = ref["gather"], ref["scatter"]

    def chosen_row(ids):
        sub = lax.broadcasted_iota(jnp.int32, (points, ov), 0).astype(F32)
        return (sub == ids).astype(F32).astype(BF16)

    def first_id(a, b):
        return float((3 * (1 - a) + (1 - b)) * points)

    def make_gather():
        for e, (a, b) in enumerate(NEAR):
            ids_col = jnp.transpose(info_all[slot(a, b), :, 0:ov])[:, 3:4] - first_id(a, b)
            lane = lax.broadcasted_iota(jnp.int32, (ov, points), 1).astype(F32)
            gather[e * ov:(e + 1) * ov, :] = (lane == ids_col).astype(F32).astype(BF16)

    def make_scatter():
        for e, (a, b) in enumerate(NEAR):
            scatter[:, e * ov:(e + 1) * ov] = chosen_row(info_all[slot(a, b), 3:4, 0:ov] - first_id(a, b))

    def borrow_first(k, h, own):
        out = ref["give_out"]
        asked = pick_dot(gather[...], packed(own))
        for e in range(8):
            a, b = NEAR[e]
            along, across = (a, b) if h == 0 else (b, a)
            out[k, h, slot(along, across)] = asked[e * ov:(e + 1) * ov]
        waits = []
        for step in BOTH:
            a, b = (step, 0) if h == 0 else (0, step)
            s = slot(step, -1)
            waits.append(send(out.at[k, h, s:s + 3], ref["take_in"].at[k, h, (1 - step) // 2], a, b))
        return waits

    def borrow_second(k, h, waits):
        for wait in waits:
            wait()
        out, came = ref["give_out"], ref["take_in"]
        waits = []
        for step in BOTH:
            mix = out.at[k, h, slot(0, step)]
            mix[...] = mix[...] + came[k, h, 0, step + 1] + came[k, h, 1, step + 1]
            a, b = (0, step) if h == 0 else (step, 0)
            waits.append(send(mix, ref["give_in"].at[k, h, (1 - step) // 2], a, b))
        return waits

    def borrow_end(k, h, waits):
        for wait in waits:
            wait()
        came, given = ref["take_in"], ref["give_in"]
        return came[k, h, 0, 1] + came[k, h, 1, 1] + given[k, h, 0] + given[k, h, 1]

    inverse = ref["inverse"]

    def precondition(k, extended, target, hooks=(), early=None, late=None):
        back, out = ref["ret"], ref["ret_out"]
        both, first = [], []
        for h in range(2):
            pack = ref["pack"].at[h]
            pack[...] = packed(extended[h])
            out[k, h] = split_dot(inverse[0, points:ext], inverse[1, points:ext], pack[...])
            waits = {}
            for a, b in ((0, 1), (0, -1), (1, 0), (-1, 0)):
                waits[a, b] = send(out.at[k, h], back.at[k, h, slot(-a, -b)], a, b)
            first.append(waits)

        def own_rows(h, carry):
            target[h] = split_dot(inverse[0, 0:points], inverse[1, 0:points], ref["pack"][h])
            return carry

        lax.fori_loop(0, 2, own_rows, 0)
        if early is not None:
            early()
        second = []
        for h in range(2):
            waits = []
            for step in BOTH:
                first[h][(0, step) if h == 0 else (step, 0)]()
            for step in BOTH:
                for other in BOTH:
                    if h == 0:
                        waits.append(send(back.at[k, h, slot(0, step)], back.at[k, h, slot(-other, step)],
                                          other, 0, guard=step))
                    else:
                        waits.append(send(back.at[k, h, slot(step, 0)], back.at[k, h, slot(step, -other)],
                                          0, other))
            for step in BOTH:
                waits.append(first[h][(step, 0) if h == 0 else (0, step)])
            second.append(waits)
        for hook in hooks:
            hook()
        if late is not None:
            late()
        for h in range(2):
            for wait in second[h]:
                wait()
            given = jnp.concatenate([packed(back[k, h, slot(a, b)]) for a, b in NEAR], axis=0)
            target[h] = target[h] + pick_dot(scatter[...], given)

    blocks = ref["blocks"]
    noise_col = ref["columns"]

    def operate(k, vector, target, hooks=(), early=None):
        halo, out, came = ref["halo"], ref["part_out"], ref["part_in"]
        waits = []
        begin = len(latest)
        for h in range(2):
            waits.append([send(vector.at[h], halo.at[k, h, (1 - step) // 2], *((step, 0) if h == 0 else (0, step)))
                          for step in BOTH])
        end = len(latest)
        noise = noise_col[1, :, 2:3]
        for h in range(2):
            ref["pack"][h, own] = packed(vector[h])

        def from_here(n, carry):
            h, t = n // 3, n % 3
            out[k, h, t] = split_dot(blocks[h, 7 - 3 * t, 0], blocks[h, 7 - 3 * t, 1], ref["pack"][h, own])
            return carry

        lax.fori_loop(0, 6, from_here, 0)
        if early is not None:
            early()
        def arrived(h, toward):
            value = None
            for source in (-1, 1):
                n = slot(toward, source)
                term = split_dot(blocks[h, n, 0], blocks[h, n, 1], sources[h][source])
                value = term if value is None else value + term
            return value

        later, sources = [], []
        for h in range(2):
            for wait in waits[h]:
                wait()
            sources.append({-1: packed(halo[k, h, 0]), 1: packed(halo[k, h, 1])})
            sends = []
            for toward in BOTH:
                part = out.at[k, h, 1 - toward]
                part[...] = part[...] + arrived(h, toward)
                a, b = (0, toward) if h == 0 else (toward, 0)
                sends.append(send(part, came.at[k, h, (1 - toward) // 2], a, b))
            later.append(sends)
        for h in range(2):
            target[h] = (out[k, h, 1] + noise * vector[h]) + arrived(h, 0)
        for hook in hooks:
            hook()
        for h in range(2):
            for wait in later[h]:
                wait()
            target[h] = target[h] + came[k, h, 0] + came[k, h, 1]
        sent(begin, end)

    sums, gathered = ref["sums"], ref["gathered"]
    counts = [many * columns_too for _, many, columns_too in groups]
    offsets = [sum(counts[:g]) for g in range(len(groups))]
    open_waits = {}

    def reduce_start(k, stage):
        waits = []
        for offset in range(1, counts[stage]):
            desc = copy_to(sums.at[k, stage], gathered.at[k, offsets[stage] + offset],
                           partner(*groups[stage], offset))
            desc.start()
            pending[0].append(desc)
            waits.append(desc.wait_recv)
        open_waits[k] = waits

    def reduce_end(k, stage):
        for wait in open_waits[k]:
            wait()
        value = sums[k, stage]
        for offset in range(1, counts[stage]):
            value = value + gathered[k, offsets[stage] + offset]
        sums[k, stage + 1] = value

    def reduce_open(k, pairs):
        rows = []
        for h in range(2):
            for left, right in pairs(h):
                rows.append(jnp.sum(left * right, axis=0, keepdims=True))
        rows.append(jnp.zeros((4, LANES), F32))
        sums[k, 0] = jnp.concatenate(rows, axis=0)
        reduce_start(k, 0)

    def reduce_next(k, stage):
        reduce_end(k, stage)
        if stage + 1 < len(groups):
            reduce_start(k, stage + 1)

    def reduced(k, h, which):
        return sums[k, len(groups), 2 * h + which:2 * h + which + 1, :]

    w0, n0, w1 = ref["w0"], ref["n0"], ref["w1"]
    z0, m0, m1, z1, n1 = ref["z0"], ref["m0"], ref["m1"], ref["z1"], ref["n1"]
    columns = ref["columns"]
    for b in (-1, 0, 1):
        columns[b + 1] = jnp.transpose(info_all[slot(0, b)])
    ids = info_all[4, 3:4, 0:ov]
    picked = jnp.zeros((32, ov), F32)
    line = lax.broadcasted_iota(jnp.int32, (8, points), 0)
    for a, b in NEAR:
        shift = jnp.where(line == 0, float(a), jnp.where(line == 1, float(b), 0.0))
        value = info_all[slot(a, b)] + shift
        high, middle = halves(value)
        low = (value - high.astype(F32) - middle.astype(F32)).astype(BF16)
        pieces = jnp.concatenate([high.astype(F32), middle.astype(F32), low.astype(F32), jnp.zeros((8, points), F32)])
        picked = picked + bf_dot(pieces.astype(BF16), chosen_row(ids - float(slot(a, b) * points)))
    picked = (picked[0:8] + picked[8:16]) + picked[16:24]
    wide = ref["wide"]
    wide[:, own] = info_all[4]
    wide[:, points:ext] = picked
    tall = ref["tall"]
    tall[...] = jnp.transpose(wide[...])
    matrix = ref["matrix"]

    def ext_rows(c, carry):
        rows = pl.ds(pl.multiple_of(c * LANES, LANES), LANES)
        value = kernel_values(tall[rows, 0:1], tall[rows, 1:2], wide[0:1, :], wide[1:2, :])
        at = lax.broadcasted_iota(jnp.int32, (LANES, ext), 0) + c * LANES
        diag = at == lax.broadcasted_iota(jnp.int32, (LANES, ext), 1)
        matrix[rows, :] = value + jnp.where(diag, wide[2:3, :], 0.0)
        return carry

    lax.fori_loop(0, ext // LANES, ext_rows, 0)

    def build(count, pair):
        def block_rows(n, carry):
            b, a = pair(n // (points // LANES))
            rows = pl.ds(pl.multiple_of(n % (points // LANES) * LANES, LANES), LANES)
            source = info_all[3 * a + 4]
            value = kernel_values(columns[b + 1, rows, 0:1], columns[b + 1, rows, 1:2],
                                  source[0:1, :] + a.astype(F32), source[1:2, :] - b.astype(F32))
            high, low = halves(value)
            blocks[0, slot(b, a), 0, rows, :] = high
            blocks[0, slot(b, a), 1, rows, :] = low
            high, low = halves(jnp.transpose(value))
            blocks[1, slot(a, b), 0, :, rows] = high
            blocks[1, slot(a, b), 1, :, rows] = low
            return carry

        lax.fori_loop(0, count * (points // LANES), block_rows, 0)

    full = ref["full"]
    at = 0
    for size in cfg["leaves"]:
        now = slice(at, at + size)
        before = slice(0, at)
        leaf, leaf_inverse = ref["leaf"].at[0:size, 0:size], ref["leaf_inverse"].at[0:size, 0:size]
        if at == 0:
            leaf[...] = matrix[now, now]
            newton_inverse(leaf, leaf_inverse)
        else:
            cross = matrix[before, now]
            reach = ref["reach"].at[0:at, 0:size]
            reach[...] = full_dot(full[before, before], cross)
            leaf[...] = matrix[now, now] - full_dot(matrix[now, before], reach[...])
            newton_inverse(leaf, leaf_inverse)
            moved = full_dot(reach[...], leaf_inverse[...])
            full[before, before] = full[before, before] + full_dot(moved, reach[...], ((1,), (1,)))
            full[before, now] = -moved
            full[now, before] = -full_dot(leaf_inverse[...], reach[...], ((1,), (1,)))
        if at == 0:
            make_gather()
            for wait in came_right:
                wait()
            waits = [borrow_first(0, h, be[h, own]) for h in range(2)]
        elif at + size == points:
            waits = [borrow_second(0, h, waits[h]) for h in range(2)]
        full[now, now] = leaf_inverse[...]
        at += size
    high, low = halves(full[...])
    inverse[0] = high
    inverse[1] = low

    for h in range(2):
        be[h, points:ext] = borrow_end(0, h, waits[h])

    precondition(0, be, z0, early=lambda: build(3, lambda n: (n - 1, 0 * n)), late=lambda: (make_scatter(), build(2, lambda n: (0 * n, 2 * n - 1))))
    operate(0, z0, w0.at[:, own], early=lambda: build(4, lambda n: (2 * (n // 2) - 1, 2 * (n % 2) - 1)))
    reduce_open(0, lambda h: ((be[h, own], z0[h]), (z0[h], w0[h, own])))

    def borrow(k, vector, hook):
        waits = [borrow_first(k, h, vector[h, own]) for h in range(2)]
        waits = [borrow_second(k, h, waits[h]) for h in range(2)]
        hook()
        for h in range(2):
            vector[h, points:ext] = borrow_end(k, h, waits[h])

    borrow(1, w0, lambda: reduce_next(0, 0))
    precondition(1, w0, m0)
    operate(1, m0, n0.at[:, own], [lambda: reduce_next(0, 1)])

    for h in range(2):
        alpha = reduced(0, h, 0) / reduced(0, h, 1)
        z1[h] = z0[h] - alpha * m0[h]
        w1[h, own] = w0[h, own] - alpha * n0[h, own]
        be[h, own] = be[h, own] - alpha * w0[h, own]
    reduce_open(1, lambda h: ((be[h, own], z1[h]), (z1[h], w1[h, own])))
    borrow(2, n0, lambda: reduce_next(1, 0))
    for h in range(2):
        alpha = reduced(0, h, 0) / reduced(0, h, 1)
        w1[h, points:ext] = w0[h, points:ext] - alpha * n0[h, points:ext]
    precondition(2, w1, m1)
    operate(2, m1, n1, [lambda: reduce_next(1, 1)])

    def steps(h):
        gamma0, delta0 = reduced(0, h, 0), reduced(0, h, 1)
        gamma1, delta1 = reduced(1, h, 0), reduced(1, h, 1)
        alpha0 = gamma0 / delta0
        beta1 = gamma1 / gamma0
        alpha1 = gamma1 / (delta1 - beta1 * gamma1 / alpha0)
        return alpha0, beta1, alpha1, gamma1

    result, got = ref["result"], ref["got"]

    for h in range(2):
        alpha0, beta1, alpha1, _ = steps(h)
        direction = z1[h] + beta1 * z0[h]
        image = w1[h, own] + beta1 * w0[h, own]
        result[0, h] = alpha0 * z0[h] + alpha1 * direction
        be[h, own] = be[h, own] - alpha1 * image
        z1[h] = z1[h] - alpha1 * (m1[h] + beta1 * m0[h])
        w1[h, own] = w1[h, own] - alpha1 * (n1[h] + beta1 * n0[h, own])
        z0[h] = direction
        w0[h, own] = image
    reduce_open(2, lambda h: ((be[h, own], z1[h]), (z1[h], w1[h, own])))
    for stage in range(len(groups)):
        reduce_next(2, stage)
    home = []
    for h in range(2):
        _, _, alpha1, gamma1 = steps(h)
        gamma2, delta2 = reduced(2, h, 0), reduced(2, h, 1)
        beta2 = gamma2 / gamma1
        alpha2 = gamma2 / (delta2 - beta2 * gamma2 / alpha1)
        result[0, h] = result[0, h] + alpha2 * (z1[h] + beta2 * z0[h])
        home.append(send(result.at[0, h], got.at[0, h], 0, 0, guard="traded", target=mate))
        result[1, h] = be[h, own] - alpha2 * (w1[h, own] + beta2 * w0[h, own])
        home.append(send(result.at[1, h], got.at[1, h], 0, 0, guard="traded", target=mate))

    @pl.when(kept)
    def _():
        for h in range(2):
            x_ref[:, half(h)] = result[0, h]
            r_ref[:, half(h)] = result[1, h]

    for n, wait in enumerate(home):
        wait()

        @pl.when(traded)
        def _():
            (x_ref, r_ref)[n % 2][:, half(n // 2)] = got[n % 2, n // 2]

    for which in (0, 1, -1, "traded"):
        def drain(descs=pending[which]):
            for desc in descs:
                desc.wait_send()
        guarded(which, drain)
    assert counter[0] <= cfg["copies"], counter[0]


def make(gx, gy, points, ov, rhs):
    ext = points + ov
    groups = ((1, 2, gy), (2, gx // 2, 1))
    each = [many * columns_too for _, many, columns_too in groups]
    copies = 8 + 7 + 3 * (16 + 8 + 8) + 3 * sum(n - 1 for n in each)
    stages = len(groups)
    half = (2, points, LANES)
    tall = (2, ext, LANES)
    shapes = {
        "send": pltpu.SemaphoreType.DMA((copies,)),
        "recv": pltpu.SemaphoreType.DMA((copies,)),
        "info_all": ((9, 8, points), F32),
        "gather": ((8 * ov, points), BF16),
        "scatter": ((points, 8 * ov), BF16),
        "ret": ((3, 2, 9, ov, LANES), F32),
        "ret_out": ((3, 2, ov, LANES), F32),
        "halo": ((3, 2, 2, points, LANES), F32),
        "part_out": ((3, 2, 3, points, LANES), F32),
        "part_in": ((3, 2, 2, points, LANES), F32),
        "give_out": ((3, 2, 9, ov, LANES), F32),
        "take_in": ((3, 2, 2, 3, ov, LANES), F32),
        "give_in": ((3, 2, 2, ov, LANES), F32),
        "pack": ((2, ext, 2 * LANES), BF16),
        "inverse": ((2, ext, ext), BF16),
        "blocks": ((2, 9, 2, points, points), BF16),
        "columns": ((3, points, 8), F32),
        "wide": ((8, ext), F32),
        "tall": ((ext, 8), F32),
        "matrix": ((ext, ext), F32),
        "full": ((ext, ext), F32),
        "leaf": ((256, 256), F32),
        "leaf_inverse": ((256, 256), F32),
        "reach": ((points, 256), F32),
        "result": ((2, 2, points, LANES), F32),
        "got": ((2, 2, points, LANES), F32),
        "sums": ((3, stages + 1, 8, LANES), F32),
        "gathered": ((3, sum(each), 8, LANES), F32),
        "be": (tall, F32), "w0": (tall, F32), "n0": (tall, F32), "w1": (tall, F32),
        "z0": (half, F32), "m0": (half, F32), "m1": (half, F32), "z1": (half, F32), "n1": (half, F32),
    }
    cfg = {"names": tuple(shapes), "points": points, "ov": ov, "gx": gx, "gy": gy, "groups": groups,
           "copies": copies, "leaves": (256,) * (points // 256) + (ov,)}
    scratch = [pltpu.VMEM(*v) if isinstance(v, tuple) else v for v in shapes.values()]
    whole = pl.BlockSpec(memory_space=pltpu.VMEM)
    call = pl.pallas_call(
        functools.partial(body, cfg),
        out_shape=(jax.ShapeDtypeStruct((points, rhs), F32),) * 2,
        in_specs=[whole, whole],
        out_specs=(whole, whole),
        scratch_shapes=scratch,
        compiler_params=pltpu.CompilerParams(
            collective_id=0, has_side_effects=True, vmem_limit_bytes=67043328),
    )

    def shards(right_side, coords, noise, intersect):
        ids = jnp.pad(intersect.reshape(1, ov).astype(F32), ((0, 0), (0, points - ov)))
        info = jnp.concatenate(
            [coords.reshape(2, points), noise.reshape(1, points), ids, jnp.zeros((4, points), F32)], axis=0)
        x, r = call(info, right_side.reshape(points, rhs))
        return x.reshape(right_side.shape), r.reshape(right_side.shape)

    return shards


def solution(mesh):
    gx, gy = mesh.shape["gx"], mesh.shape["gy"]

    def run(right_side, coords, noise, intersect):
        points, rhs = right_side.shape[2:]
        spec4, spec3 = P("gx", "gy", None, None), P("gx", "gy", None)
        return jax.shard_map(
            make(gx, gy, points, intersect.shape[2], rhs), mesh=mesh,
            in_specs=(spec4, spec4, spec3, spec3), out_specs=(spec4, spec4), check_vma=False,
        )(right_side, coords, noise, intersect)

    return run
```

profile of v0, /device:TPU:24, one launch (start us, length us, event | category | flops | bytes accessed | tf_op | source)
XLA Modules:
  0.0 189.9 jit_solution(7655549422985987233)
XLA Ops:
  0.6 0.0 copy-start.3
  0.6 0.0 copy-start.1
  0.6 0.6 copy-done.3
  1.3 0.0 copy-start.2
  1.3 0.1 pad.8.clone
  1.4 0.0 copy-done.1
  1.4 0.6 copy-done.2
  2.0 0.7 fusion.info_ref
  2.6 184.5 %shard_map.59 = (f32[512,256]{1,0:T(8,128)}, f32[512,256]{1,0:T(8,128)}) custom-call(f32[8,512]{1,0:T(8,128)} %fusion.info_ref, f32[512,256]{1,0:T(8,128)} %bitcast.7), custom_call_target="tpu_custom_call" | custom-call | tf_op jit(solution)/shard_map/pallas_call | solution.py:634
  187.2 0.0 copy-start
  187.2 1.9 %copy.8 = f32[1,1,512,256]{3,2,1,0:T(8,128)} copy(f32[1,1,512,256]{3,2,1,0:T(8,128)} %bitcast.9) | data formatting | bytes 1048576
  189.1 0.0 copy-done
  189.1 0.8 copy.9
  (2 shorter events, 0.0 us)
Async XLA Ops:
  0.6 0.7 copy-start.3
  0.6 0.7 copy-start.1
  1.3 0.7 copy-start.2
  187.2 1.9 %copy-start = (f32[512,256]{1,0:T(8,128)S(1)}, f32[512,256]{1,0:T(8,128)}, u32[]{:S(2)}) copy-start(f32[512,256]{1,0:T(8,128)} %get-tuple-element.5) | copy-start | bytes 1572868
where the time goes:
time: 190 us
  Pallas kernels  185 us (97%)
  local copies, waits for them, and re-layouts  4.04 us (2%)
    pallas_call x1, Pallas kernels, shards(): x, r = call(info, right_side.reshape(points, rhs))  185 us
    unnamed x10, local copies, waits for them, and re-layouts  3.96 us

commit v1 on v0

--- a/solution.py
+++ b/solution.py
@@ -96,7 +96,7 @@
     step(full_dot, least)
 
 
-def body(cfg, info_ref, b_ref, x_ref, r_ref, *scratch):
+def body(cfg, coords_ref, noise_ref, ids_ref, b_ref, x_ref, r_ref, *scratch):
     ref = dict(zip(cfg["names"], scratch))
     points, ov = cfg["points"], cfg["ov"]
     ext = points + ov
@@ -155,6 +155,12 @@
         for out, desc in latest[begin:end]:
             guarded(out, desc.wait_send)
             pending[out][:] = [other for other in pending[out] if other is not desc]
+
+    info_ref = ref["info"]
+    info_ref[...] = jnp.concatenate([
+        coords_ref[...], noise_ref[...],
+        jnp.concatenate([ids_ref[...].astype(F32), jnp.zeros((1, points - ov), F32)], axis=1),
+        jnp.zeros((4, points), F32)], axis=0)
 
     info_all = ref["info_all"]
     for n in range(9):
@@ -267,7 +273,7 @@
 
     inverse = ref["inverse"]
 
-    def precondition(k, extended, target, hooks=(), early=None, late=None):
+    def precondition(k, extended, target, early=None, late=None):
         back, out = ref["ret"], ref["ret_out"]
         both, first = [], []
         for h in range(2):
@@ -302,27 +308,24 @@
             for step in BOTH:
                 waits.append(first[h][(step, 0) if h == 0 else (0, step)])
             second.append(waits)
-        for hook in hooks:
-            hook()
         if late is not None:
             late()
+        begin, leaving = len(latest), []
         for h in range(2):
             for wait in second[h]:
                 wait()
             given = jnp.concatenate([packed(back[k, h, slot(a, b)]) for a, b in NEAR], axis=0)
             target[h] = target[h] + pick_dot(scatter[...], given)
+            leaving.append([send(target.at[h], ref["halo"].at[k, h, (1 - step) // 2],
+                                 *((step, 0) if h == 0 else (0, step))) for step in BOTH])
+        return leaving, begin, len(latest)
 
     blocks = ref["blocks"]
     noise_col = ref["columns"]
 
-    def operate(k, vector, target, hooks=(), early=None):
+    def operate(k, vector, target, started, hooks=(), early=None):
         halo, out, came = ref["halo"], ref["part_out"], ref["part_in"]
-        waits = []
-        begin = len(latest)
-        for h in range(2):
-            waits.append([send(vector.at[h], halo.at[k, h, (1 - step) // 2], *((step, 0) if h == 0 else (0, step)))
-                          for step in BOTH])
-        end = len(latest)
+        waits, begin, end = started
         noise = noise_col[1, :, 2:3]
         for h in range(2):
             ref["pack"][h, own] = packed(vector[h])
@@ -335,34 +338,46 @@
         lax.fori_loop(0, 6, from_here, 0)
         if early is not None:
             early()
-        def arrived(h, toward):
+        sources = ref["sources"]
+        piece = points // 2
+
+        def arrived(h, toward, rows):
             value = None
-            for source in (-1, 1):
-                n = slot(toward, source)
-                term = split_dot(blocks[h, n, 0], blocks[h, n, 1], sources[h][source])
+            for n, source in enumerate((-1, 1)):
+                at = (toward + 1) * 3 + source + 1
+                term = split_dot(blocks[h, at, 0, rows, :], blocks[h, at, 1, rows, :], sources[h, n])
                 value = term if value is None else value + term
             return value
 
-        later, sources = [], []
+        def hand_on(h, rows):
+            for toward in BOTH:
+                part = out.at[k, h, 1 - toward, rows]
+                part[...] = part[...] + arrived(h, toward, rows)
+                a, b = (0, toward) if h == 0 else (toward, 0)
+                later[h].append(send(part, came.at[k, h, (1 - toward) // 2, rows], a, b))
+
+        later = [[], []]
         for h in range(2):
             for wait in waits[h]:
                 wait()
-            sources.append({-1: packed(halo[k, h, 0]), 1: packed(halo[k, h, 1])})
-            sends = []
-            for toward in BOTH:
-                part = out.at[k, h, 1 - toward]
-                part[...] = part[...] + arrived(h, toward)
-                a, b = (0, toward) if h == 0 else (toward, 0)
-                sends.append(send(part, came.at[k, h, (1 - toward) // 2], a, b))
-            later.append(sends)
-        for h in range(2):
-            target[h] = (out[k, h, 1] + noise * vector[h]) + arrived(h, 0)
+            for n in range(2):
+                sources[h, n] = packed(halo[k, h, n])
+            hand_on(h, slice(0, piece))
+        for h in range(2):
+            hand_on(h, slice(piece, points))
+
+        def own_sums(n, carry):
+            h, rows = n // 2, pl.ds(pl.multiple_of(n % 2 * piece, piece), piece)
+            out[k, h, 1, rows, :] = out[k, h, 1, rows, :] + arrived(h, 0, rows)
+            return carry
+
+        lax.fori_loop(0, 4, own_sums, 0)
         for hook in hooks:
             hook()
         for h in range(2):
             for wait in later[h]:
                 wait()
-            target[h] = target[h] + came[k, h, 0] + came[k, h, 1]
+            target[h] = (out[k, h, 1] + noise * vector[h]) + (came[k, h, 0] + came[k, h, 1])
         sent(begin, end)
 
     sums, gathered = ref["sums"], ref["gathered"]
@@ -490,33 +505,38 @@
     for h in range(2):
         be[h, points:ext] = borrow_end(0, h, waits[h])
 
-    precondition(0, be, z0, early=lambda: build(3, lambda n: (n - 1, 0 * n)), late=lambda: (make_scatter(), build(2, lambda n: (0 * n, 2 * n - 1))))
-    operate(0, z0, w0.at[:, own], early=lambda: build(4, lambda n: (2 * (n // 2) - 1, 2 * (n % 2) - 1)))
-    reduce_open(0, lambda h: ((be[h, own], z0[h]), (z0[h], w0[h, own])))
-
-    def borrow(k, vector, hook):
+    started = precondition(0, be, z0, early=lambda: build(3, lambda n: (n - 1, 0 * n)),
+                           late=lambda: (make_scatter(), build(2, lambda n: (0 * n, 2 * n - 1))))
+    operate(0, z0, w0.at[:, own], started,
+            early=lambda: build(4, lambda n: (2 * (n // 2) - 1, 2 * (n % 2) - 1)))
+
+    def borrow(k, vector, between):
         waits = [borrow_first(k, h, vector[h, own]) for h in range(2)]
+        between()
         waits = [borrow_second(k, h, waits[h]) for h in range(2)]
-        hook()
         for h in range(2):
             vector[h, points:ext] = borrow_end(k, h, waits[h])
 
-    borrow(1, w0, lambda: reduce_next(0, 0))
-    precondition(1, w0, m0)
-    operate(1, m0, n0.at[:, own], [lambda: reduce_next(0, 1)])
-
-    for h in range(2):
-        alpha = reduced(0, h, 0) / reduced(0, h, 1)
-        z1[h] = z0[h] - alpha * m0[h]
-        w1[h, own] = w0[h, own] - alpha * n0[h, own]
-        be[h, own] = be[h, own] - alpha * w0[h, own]
-    reduce_open(1, lambda h: ((be[h, own], z1[h]), (z1[h], w1[h, own])))
-    borrow(2, n0, lambda: reduce_next(1, 0))
+    borrow(1, w0, lambda: reduce_open(0, lambda h: ((be[h, own], z0[h]), (z0[h], w0[h, own]))))
+    started = precondition(1, w0, m0)
+    reduce_next(0, 0)
+    operate(1, m0, n0.at[:, own], started, [lambda: reduce_next(0, 1)])
+
+    def first_step():
+        for h in range(2):
+            alpha = reduced(0, h, 0) / reduced(0, h, 1)
+            z1[h] = z0[h] - alpha * m0[h]
+            w1[h, own] = w0[h, own] - alpha * n0[h, own]
+            be[h, own] = be[h, own] - alpha * w0[h, own]
+        reduce_open(1, lambda h: ((be[h, own], z1[h]), (z1[h], w1[h, own])))
+
+    borrow(2, n0, first_step)
     for h in range(2):
         alpha = reduced(0, h, 0) / reduced(0, h, 1)
         w1[h, points:ext] = w0[h, points:ext] - alpha * n0[h, points:ext]
-    precondition(2, w1, m1)
-    operate(2, m1, n1, [lambda: reduce_next(1, 1)])
+    started = precondition(2, w1, m1)
+    reduce_next(1, 0)
+    operate(2, m1, n1, started, [lambda: reduce_next(1, 1)])
 
     def steps(h):
         gamma0, delta0 = reduced(0, h, 0), reduced(0, h, 1)
@@ -577,13 +597,14 @@
     ext = points + ov
     groups = ((1, 2, gy), (2, gx // 2, 1))
     each = [many * columns_too for _, many, columns_too in groups]
-    copies = 8 + 7 + 3 * (16 + 8 + 8) + 3 * sum(n - 1 for n in each)
+    copies = 8 + 7 + 3 * (16 + 12 + 8) + 3 * sum(n - 1 for n in each)
     stages = len(groups)
     half = (2, points, LANES)
     tall = (2, ext, LANES)
     shapes = {
         "send": pltpu.SemaphoreType.DMA((copies,)),
         "recv": pltpu.SemaphoreType.DMA((copies,)),
+        "info": ((8, points), F32),
         "info_all": ((9, 8, points), F32),
         "gather": ((8 * ov, points), BF16),
         "scatter": ((points, 8 * ov), BF16),
@@ -598,6 +619,7 @@
         "pack": ((2, ext, 2 * LANES), BF16),
         "inverse": ((2, ext, ext), BF16),
         "blocks": ((2, 9, 2, points, points), BF16),
+        "sources": ((2, 2, points, 2 * LANES), BF16),
         "columns": ((3, points, 8), F32),
         "wide": ((8, ext), F32),
         "tall": ((ext, 8), F32),
@@ -620,7 +642,7 @@
     call = pl.pallas_call(
         functools.partial(body, cfg),
         out_shape=(jax.ShapeDtypeStruct((points, rhs), F32),) * 2,
-        in_specs=[whole, whole],
+        in_specs=[whole] * 4,
         out_specs=(whole, whole),
         scratch_shapes=scratch,
         compiler_params=pltpu.CompilerParams(
@@ -628,10 +650,8 @@
     )
 
     def shards(right_side, coords, noise, intersect):
-        ids = jnp.pad(intersect.reshape(1, ov).astype(F32), ((0, 0), (0, points - ov)))
-        info = jnp.concatenate(
-            [coords.reshape(2, points), noise.reshape(1, points), ids, jnp.zeros((4, points), F32)], axis=0)
-        x, r = call(info, right_side.reshape(points, rhs))
+        x, r = call(coords.reshape(2, points), noise.reshape(1, points), intersect.reshape(1, ov),
+                    right_side.reshape(points, rhs))
         return x.reshape(right_side.shape), r.reshape(right_side.shape)
 
     return shards

time: 190 us -> 185 us (0.974)
  Pallas kernels: 185 us -> 182 us
    pallas_call x1, Pallas kernels: 185 us -> 182 us  [shards(): call(coords.reshape(2, points), noise.reshape(1, points), intersect.resha...]
    unnamed x10 -> x4, local copies, waits for them, and re-layouts: 3.96 us -> 2.72 us
where the time goes in v1:
time: 185 us
  Pallas kernels  182 us (98%)
  local copies, waits for them, and re-layouts  2.72 us (1%)
    pallas_call x1, Pallas kernels, shards(): call(coords.reshape(2, points), noise.reshape(1, points), intersect.resha...  182 us

profile of v1, /device:TPU:24, one launch (start us, length us, event | category | flops | bytes accessed | tf_op | source)
XLA Modules:
  0.0 184.9 jit_solution(1388373091694870047)
XLA Ops:
  0.6 181.5 %shard_map.59 = (f32[512,256]{1,0:T(8,128)}, f32[512,256]{1,0:T(8,128)}) custom-call(f32[2,512]{1,0:T(2,128)} %bitcast.9, f32[1,512]{1,0:T(1,128)} %bitcast.10, s32[1,128]{1,0:T(1,128)} %bitcast.11, f32[512,256]{1,0:T(8,128)} %bitcast.6), custom_call_target="tpu_custom_call" | custom-call | tf_op jit(solution)/shard_map/pallas_call | solution.py:653
  182.1 0.0 copy-start
  182.2 1.9 %copy.8 = f32[1,1,512,256]{3,2,1,0:T(8,128)} copy(f32[1,1,512,256]{3,2,1,0:T(8,128)} %bitcast.8) | data formatting | bytes 1048576
  184.1 0.0 copy-done
  184.1 0.8 copy.9
Async XLA Ops:
  182.1 1.9 %copy-start = (f32[512,256]{1,0:T(8,128)S(1)}, f32[512,256]{1,0:T(8,128)}, u32[]{:S(2)}) copy-start(f32[512,256]{1,0:T(8,128)} %get-tuple-element.5) | copy-start | bytes 1572868

commit v2 on v1

--- a/solution.py
+++ b/solution.py
@@ -185,10 +185,13 @@
 
     groups = cfg["groups"]
 
-    def partner(stride, many, columns_too, offset):
-        position = (seat // stride) % many
-        ahead = (position + offset % many) % many
-        return (seat + (ahead - position) * stride, (col + offset // many) % gy if columns_too > 1 else col)
+    def partner(group, offset):
+        line, pair, core = seat // 4, (seat // 2) % 2, seat % 2
+        if group == "plane":
+            pair, other = (pair + offset % 2) % 2, (col + offset // 2) % gy
+            return (4 * line + 2 * pair + core, other)
+        core, line = (core + offset % 2) % 2, (line + offset // 2) % (gx // 4)
+        return (4 * line + 2 * pair + core, col)
 
     barrier = pltpu.get_barrier_semaphore()
     for a, b in NEAR:
@@ -197,8 +200,8 @@
     pl.semaphore_signal(barrier, inc=1, device_id=mate, device_id_type=MESH)
     total = 3 * len(NEAR) + 1
     for group in groups:
-        for offset in range(1, group[1] * group[2]):
-            pl.semaphore_signal(barrier, inc=1, device_id=partner(*group, offset), device_id_type=MESH)
+        for offset in range(1, group[1]):
+            pl.semaphore_signal(barrier, inc=1, device_id=partner(group[0], offset), device_id_type=MESH)
             total += 1
     pl.semaphore_wait(barrier, total)
 
@@ -381,7 +384,7 @@
         sent(begin, end)
 
     sums, gathered = ref["sums"], ref["gathered"]
-    counts = [many * columns_too for _, many, columns_too in groups]
+    counts = [count for _, count in groups]
     offsets = [sum(counts[:g]) for g in range(len(groups))]
     open_waits = {}
 
@@ -389,7 +392,7 @@
         waits = []
         for offset in range(1, counts[stage]):
             desc = copy_to(sums.at[k, stage], gathered.at[k, offsets[stage] + offset],
-                           partner(*groups[stage], offset))
+                           partner(groups[stage][0], offset))
             desc.start()
             pending[0].append(desc)
             waits.append(desc.wait_recv)
@@ -536,7 +539,6 @@
         w1[h, points:ext] = w0[h, points:ext] - alpha * n0[h, points:ext]
     started = precondition(2, w1, m1)
     reduce_next(1, 0)
-    operate(2, m1, n1, started, [lambda: reduce_next(1, 1)])
 
     def steps(h):
         gamma0, delta0 = reduced(0, h, 0), reduced(0, h, 1)
@@ -548,16 +550,21 @@
 
     result, got = ref["result"], ref["got"]
 
+    def second_step():
+        for h in range(2):
+            alpha0, beta1, alpha1, _ = steps(h)
+            direction = z1[h] + beta1 * z0[h]
+            image = w1[h, own] + beta1 * w0[h, own]
+            result[0, h] = alpha0 * z0[h] + alpha1 * direction
+            be[h, own] = be[h, own] - alpha1 * image
+            z1[h] = z1[h] - alpha1 * (m1[h] + beta1 * m0[h])
+            w1[h, own] = w1[h, own] - (alpha1 * beta1) * n0[h, own]
+            z0[h] = direction
+            w0[h, own] = image
+
+    operate(2, m1, n1, started, [lambda: reduce_next(1, 1), second_step])
     for h in range(2):
-        alpha0, beta1, alpha1, _ = steps(h)
-        direction = z1[h] + beta1 * z0[h]
-        image = w1[h, own] + beta1 * w0[h, own]
-        result[0, h] = alpha0 * z0[h] + alpha1 * direction
-        be[h, own] = be[h, own] - alpha1 * image
-        z1[h] = z1[h] - alpha1 * (m1[h] + beta1 * m0[h])
-        w1[h, own] = w1[h, own] - alpha1 * (n1[h] + beta1 * n0[h, own])
-        z0[h] = direction
-        w0[h, own] = image
+        w1[h, own] = w1[h, own] - steps(h)[2] * n1[h]
     reduce_open(2, lambda h: ((be[h, own], z1[h]), (z1[h], w1[h, own])))
     for stage in range(len(groups)):
         reduce_next(2, stage)
@@ -595,8 +602,8 @@
 
 def make(gx, gy, points, ov, rhs):
     ext = points + ov
-    groups = ((1, 2, gy), (2, gx // 2, 1))
-    each = [many * columns_too for _, many, columns_too in groups]
+    groups = (("plane", 2 * gy), ("line", gx // 2))
+    each = [count for _, count in groups]
     copies = 8 + 7 + 3 * (16 + 12 + 8) + 3 * sum(n - 1 for n in each)
     stages = len(groups)
     half = (2, points, LANES)

time: 185 us -> 186 us (level)
  no operation moved by 1% of the time
where the time goes in v2:
time: 186 us; the launch traced here: 184 us
  Pallas kernels  181 us (97%)
  local copies, waits for them, and re-layouts  2.72 us (1%)
    pallas_call x1, Pallas kernels, shards(): call(coords.reshape(2, points), noise.reshape(1, points), intersect.resha...  181 us

profile of v2, /device:TPU:24, one launch (start us, length us, event | category | flops | bytes accessed | tf_op | source)
XLA Modules:
  0.0 184.3 jit_solution(14267573969148456090)
XLA Ops:
  0.6 181.0 %shard_map.59 = (f32[512,256]{1,0:T(8,128)}, f32[512,256]{1,0:T(8,128)}) custom-call(f32[2,512]{1,0:T(2,128)} %bitcast.9, f32[1,512]{1,0:T(1,128)} %bitcast.10, s32[1,128]{1,0:T(1,128)} %bitcast.11, f32[512,256]{1,0:T(8,128)} %bitcast.6), custom_call_target="tpu_custom_call" | custom-call | tf_op jit(solution)/shard_map/pallas_call | solution.py:660
  181.6 0.0 copy-start
  181.6 1.9 %copy.8 = f32[1,1,512,256]{3,2,1,0:T(8,128)} copy(f32[1,1,512,256]{3,2,1,0:T(8,128)} %bitcast.8) | data formatting | bytes 1048576
  183.5 0.0 copy-done
  183.6 0.8 copy.9
Async XLA Ops:
  181.6 1.9 %copy-start = (f32[512,256]{1,0:T(8,128)S(1)}, f32[512,256]{1,0:T(8,128)}, u32[]{:S(2)}) copy-start(f32[512,256]{1,0:T(8,128)} %get-tuple-element.5) | copy-start | bytes 1572868

commit v3 on v2

--- a/solution.py
+++ b/solution.py
@@ -549,6 +549,7 @@
         return alpha0, beta1, alpha1, gamma1
 
     result, got = ref["result"], ref["got"]
+    home = [[], []]
 
     def second_step():
         for h in range(2):
@@ -561,6 +562,8 @@
             w1[h, own] = w1[h, own] - (alpha1 * beta1) * n0[h, own]
             z0[h] = direction
             w0[h, own] = image
+            for n, piece in enumerate((result.at[0, h], z1.at[h], z0.at[h])):
+                home[h].append(send(piece, got.at[n, h], 0, 0, guard="traded", target=mate))
 
     operate(2, m1, n1, started, [lambda: reduce_next(1, 1), second_step])
     for h in range(2):
@@ -568,29 +571,33 @@
     reduce_open(2, lambda h: ((be[h, own], z1[h]), (z1[h], w1[h, own])))
     for stage in range(len(groups)):
         reduce_next(2, stage)
-    home = []
     for h in range(2):
         _, _, alpha1, gamma1 = steps(h)
         gamma2, delta2 = reduced(2, h, 0), reduced(2, h, 1)
         beta2 = gamma2 / gamma1
         alpha2 = gamma2 / (delta2 - beta2 * gamma2 / alpha1)
-        result[0, h] = result[0, h] + alpha2 * (z1[h] + beta2 * z0[h])
-        home.append(send(result.at[0, h], got.at[0, h], 0, 0, guard="traded", target=mate))
         result[1, h] = be[h, own] - alpha2 * (w1[h, own] + beta2 * w0[h, own])
-        home.append(send(result.at[1, h], got.at[1, h], 0, 0, guard="traded", target=mate))
-
-    @pl.when(kept)
-    def _():
-        for h in range(2):
-            x_ref[:, half(h)] = result[0, h]
+        last = send(result.at[1, h], got.at[3, h], 0, 0, guard="traded", target=mate)
+
+        @pl.when(kept)
+        def _():
+            x_ref[:, half(h)] = result[0, h] + alpha2 * (z1[h] + beta2 * z0[h])
             r_ref[:, half(h)] = result[1, h]
 
-    for n, wait in enumerate(home):
-        wait()
+        for wait in home[h]:
+            wait()
 
         @pl.when(traded)
         def _():
-            (x_ref, r_ref)[n % 2][:, half(n // 2)] = got[n % 2, n // 2]
+            x_ref[:, half(h)] = got[0, h] + alpha2 * (got[1, h] + beta2 * got[2, h])
+
+        home[h] = last
+    for h in range(2):
+        home[h]()
+
+        @pl.when(traded)
+        def _():
+            r_ref[:, half(h)] = got[3, h]
 
     for which in (0, 1, -1, "traded"):
         def drain(descs=pending[which]):
@@ -604,7 +611,7 @@
     ext = points + ov
     groups = (("plane", 2 * gy), ("line", gx // 2))
     each = [count for _, count in groups]
-    copies = 8 + 7 + 3 * (16 + 12 + 8) + 3 * sum(n - 1 for n in each)
+    copies = 8 + 3 + 8 + 3 * (16 + 12 + 8) + 3 * sum(n - 1 for n in each)
     stages = len(groups)
     half = (2, points, LANES)
     tall = (2, ext, LANES)
@@ -636,7 +643,7 @@
         "leaf_inverse": ((256, 256), F32),
         "reach": ((points, 256), F32),
         "result": ((2, 2, points, LANES), F32),
-        "got": ((2, 2, points, LANES), F32),
+        "got": ((4, 2, points, LANES), F32),
         "sums": ((3, stages + 1, 8, LANES), F32),
         "gathered": ((3, sum(each), 8, LANES), F32),
         "be": (tall, F32), "w0": (tall, F32), "n0": (tall, F32), "w1": (tall, F32),

time: 186 us -> 194 us (1.043)
  Pallas kernels: 181 us -> 188 us
    pallas_call x1, Pallas kernels: 181 us -> 188 us  [shards(): call(coords.reshape(2, points), noise.reshape(1, points), intersect.resha...]
where the time goes in v3:
time: 194 us; the launch traced here: 191 us
  Pallas kernels  188 us (97%)
  local copies, waits for them, and re-layouts  2.72 us (1%)
    pallas_call x1, Pallas kernels, shards(): call(coords.reshape(2, points), noise.reshape(1, points), intersect.resha...  188 us

profile of v3, /device:TPU:24, one launch (start us, length us, event | category | flops | bytes accessed | tf_op | source)
XLA Modules:
  0.0 191.3 jit_solution(3926343180123210453)
XLA Ops:
  0.6 187.9 %shard_map.59 = (f32[512,256]{1,0:T(8,128)}, f32[512,256]{1,0:T(8,128)}) custom-call(f32[2,512]{1,0:T(2,128)} %bitcast.9, f32[1,512]{1,0:T(1,128)} %bitcast.10, s32[1,128]{1,0:T(1,128)} %bitcast.11, f32[512,256]{1,0:T(8,128)} %bitcast.6), custom_call_target="tpu_custom_call" | custom-call | tf_op jit(solution)/shard_map/pallas_call | solution.py:667
  188.6 0.0 copy-start
  188.6 1.9 %copy.8 = f32[1,1,512,256]{3,2,1,0:T(8,128)} copy(f32[1,1,512,256]{3,2,1,0:T(8,128)} %bitcast.8) | data formatting | bytes 1048576
  190.5 0.0 copy-done
  190.5 0.8 copy.9
Async XLA Ops:
  188.6 1.9 %copy-start = (f32[512,256]{1,0:T(8,128)S(1)}, f32[512,256]{1,0:T(8,128)}, u32[]{:S(2)}) copy-start(f32[512,256]{1,0:T(8,128)} %get-tuple-element.5) | copy-start | bytes 1572868
